TPU v7x, 32 devices: a whole 2x2x4 slice. The times are simulated.
32 devices in a mesh: grp: 8 (over y, x, core), dom: 4 (over z).
Axes of the slice: x: 2, y: 2, z: 4, core: 2. Of those that a mesh axis runs over, the one named last changes fastest.
Arguments:
- surplus: float32 [128, 512, 512], P('grp', 'dom'), may hold values from -0.4 to 0.4
- block_ids: int32 [128, 512], P('grp', 'dom'), may hold values from 0 to 4095, as said below
- coef: int32 [128], P('grp'), may hold values from -4 to 6, as said below
Outputs:
- updated: float32 [128, 512, 512], P('grp', 'dom')
Inputs may be any that keep to these rules, and one draw needn't show every extreme that they name: `block_ids`: for each grid, the slots in columns d * 128 to (d + 1) * 128 - 1 hold 128 different numbers from d * 1024 to (d + 1) * 1024 - 1. `coef`: each coefficient is one of 1, -4, 6.
All inputs are finite; a program needn't handle non-finite values.
Results may differ from a plain program's by a relative error of at most 0.000071.
Values sent between devices are 32-bit elements; how exact they have to be, the bound alone decides.
A program may use at most 64 MiB of HBM per device.

v0:
```python
import jax
import jax.numpy as jnp
from jax import lax
from jax.sharding import PartitionSpec as P

NBD = 1024


def local(surplus, block_ids, coef):
    offset = lax.axis_index("dom") * NBD
    local_ids = block_ids - offset
    columns = lax.broadcasted_iota(jnp.int32, (1, 1, NBD), 2)
    onehot = (local_ids[:, :, None] == columns).astype(jnp.float32)
    scaled = surplus * coef.astype(jnp.float32)[:, None, None]
    partial_sum = jnp.einsum("gkn,gkb->nb", onehot, scaled, precision=lax.Precision.HIGHEST)
    combined = lax.psum(partial_sum, "grp")
    return jnp.einsum("gkn,nb->gkb", onehot, combined, precision=lax.Precision.HIGHEST)


def solution(mesh):
    return jax.shard_map(
        local,
        mesh=mesh,
        in_specs=(P("grp", "dom", None), P("grp", "dom"), P("grp")),
        out_specs=P("grp", "dom", None),
        check_vma=False,
    )
```

profile of v0, /device:TPU:0, one launch (start us, length us, event | category | flops | bytes accessed | tf_op | source)
XLA Modules:
  0.0 106.6 jit_solution(6642148042508687133)
XLA Ops:
  6.5 0.0 all-reduce.2.cloned.1.call-start
  6.5 0.7 convert_element_type.4
  7.2 0.7 broadcast_subtract_fusion
  7.9 16.8 %fusion.7 = f32[1024,512]{1,0:T(8,128)} fusion(f32[16,128,512]{2,1,0:T(8,128)} %param.3, f32[16]{0:T(128)S(1)} %convert_element_type.4, s32[16,128]{1,0:T(8,128)S(1)} %broadcast_subtract_fusion), kind=kOutput, calls=%fused_computation.8 | convolution fusion | flops 12888047616 | bytes 6299712 | tf_op jit(solution)/shard_map/gkn,gkb->nb/dot_general | solution.py:15
  24.7 0.0 all-reduce.2.cloned.1.call-update
  24.7 64.6 %all-reduce.2.cloned.1.call-done = f32[1024,512]{1,0:T(8,128)} async-done(((f32[1024,512]{1,0:T(8,128)}), f32[1024,512]{1,0:T(8,128)}) %all-reduce.2.cloned.1.call-update) | async-done | bytes 2097168 | tf_op jit(solution)/shard_map/psum | solution.py:16
  89.3 10.4 %fusion = f32[16,128,512]{2,1,0:T(8,128)} fusion(s32[16,128]{1,0:T(8,128)S(1)} %broadcast_subtract_fusion, f32[1024,512]{1,0:T(8,128)} %all-reduce.2.cloned.1.call-done), kind=kOutput, calls=%fused_computation.1 | convolution fusion | flops 12886999040 | bytes 6299648 | tf_op jit(solution)/shard_map/gkn,nb->gkb/dot_general | solution.py:17
Async XLA Ops:
  6.5 82.8 %all-reduce.2.cloned.1.call-start = ((), (), s32[]{:S(2)}) async-start(), calls=%async_computation | async-start | bytes 4194304 | tf_op jit(solution)/shard_map/psum | solution.py:16
Sparse Core Ops, SparseCore 0:
  24.8 64.4 all-reduce.1
where the time goes:
time: 107 us
  waiting for transfers between devices  64.7 us (60%)
  matrix products  27.2 us (25%)
  between operations  13.4 us (13%)
  other arithmetic  1.36 us (1%)
    psum x1, waiting for transfers between devices, local(): combined = lax.psum(partial_sum, 'grp')  64.6 us
    dot_general x1, matrix products, local(): jnp.einsum('gkn,gkb->nb', onehot, scaled, precision=lax.Precision.HIGHEST)  16.8 us
    dot_general x1, matrix products, local(): jnp.einsum('gkn,nb->gkb', onehot, combined, precision=lax.Precision.HIGHEST)  10.4 us
  transfers between devices with their start and end apart: 1, of which 1 were waited for; matrix products, arithmetic and copies ran while one was open for 0% of the time, Pallas kernels for 0%

commit v1 on v0

--- a/solution.py
+++ b/solution.py
@@ -4,6 +4,17 @@
 from jax.sharding import PartitionSpec as P
 
 NBD = 1024
+
+
+def _wait_set(t0):
+    p_count = lax.axis_size("grp")
+    k_now = t0
+    upper = lambda row_out: [(j0, j0 ^ row_out) for j0 in range(p_count)]
+    for d in range(p_count.bit_length() - 1):
+        later = upper(1 << d)
+        fresh = lax.ppermute(k_now, "grp", later)
+        k_now = k_now + fresh
+    return k_now
 
 
 def local(surplus, block_ids, coef):
@@ -13,7 +24,7 @@
     onehot = (local_ids[:, :, None] == columns).astype(jnp.float32)
     scaled = surplus * coef.astype(jnp.float32)[:, None, None]
     partial_sum = jnp.einsum("gkn,gkb->nb", onehot, scaled, precision=lax.Precision.HIGHEST)
-    combined = lax.psum(partial_sum, "grp")
+    combined = _wait_set(partial_sum)
     return jnp.einsum("gkn,nb->gkb", onehot, combined, precision=lax.Precision.HIGHEST)
 
 

time: 107 us -> 128 us (1.20)
  waiting for transfers between devices: 64.7 us -> 95 us
  between operations: 13.4 us -> 0.02 us
  starting transfers between devices: 0.01 us -> 5.3 us
  matrix products: 27.2 us -> 24.7 us
    ppermute x0 -> x3, waiting for transfers between devices: none -> 95 us  [_wait_set(): fresh = lax.ppermute(k_now, 'grp', later)]
    psum x1 -> x0, waiting for transfers between devices: 64.6 us -> none  [local(): combined = lax.psum(partial_sum, 'grp')]
    ppermute x0 -> x3, starting transfers between devices: none -> 5.3 us  [_wait_set(): fresh = lax.ppermute(k_now, 'grp', later)]
    dot_general x1, matrix products: 10.4 us -> 8.48 us  [local(): jnp.einsum('gkn,nb->gkb', onehot, combined, precision=lax.Precision.HIGHEST)]
  transfers between devices with their start and end apart: 1 -> 3, of which waited for: 1 -> 3; matrix products, arithmetic and copies ran while one was open for 0% -> 0% of each run, Pallas kernels for 0% -> 0%
where the time goes in v1:
time: 128 us; the launch traced here: 127 us
  waiting for transfers between devices  95 us (74%)
  matrix products  24.7 us (19%)
  starting transfers between devices  5.3 us (4%)
  other arithmetic  2.31 us (2%)
    ppermute x3, waiting for transfers between devices, _wait_set(): fresh = lax.ppermute(k_now, 'grp', later)  95 us
    dot_general x1, matrix products, local(): jnp.einsum('gkn,gkb->nb', onehot, scaled, precision=lax.Precision.HIGHEST)  16.3 us
    dot_general x1, matrix products, local(): jnp.einsum('gkn,nb->gkb', onehot, combined, precision=lax.Precision.HIGHEST)  8.48 us
    ppermute x3, starting transfers between devices, _wait_set(): fresh = lax.ppermute(k_now, 'grp', later)  5.3 us
  transfers between devices with their start and end apart: 3, of which 3 were waited for; matrix products, arithmetic and copies ran while one was open for 0% of the time, Pallas kernels for 0%

profile of v1, /device:TPU:0, one launch (start us, length us, event | category | flops | bytes accessed | tf_op | source)
XLA Modules:
  0.0 127.4 jit_solution(6808424795790659561)
XLA Ops:
  0.0 0.7 convert_element_type.4
  0.7 0.7 broadcast_subtract_fusion
  1.4 16.3 %fusion.8 = f32[1024,512]{1,0:T(8,128)S(1)} fusion(f32[16,128,512]{2,1,0:T(8,128)} %param.3, f32[16]{0:T(128)S(1)} %convert_element_type.4, s32[16,128]{1,0:T(8,128)S(1)} %broadcast_subtract_fusion), kind=kOutput, calls=%fused_computation.9 | convolution fusion | flops 12888047616 | bytes 6299712 | tf_op jit(solution)/shard_map/gkn,gkb->nb/dot_general | solution.py:26
  17.6 0.6 collective-permute-start
  18.2 3.8 %collective-permute-done = f32[1024,512]{1,0:T(8,128)S(1)} collective-permute-done((f32[1024,512]{1,0:T(8,128)S(1)}, f32[1024,512]{1,0:T(8,128)S(1)}, u32[]{:S(2)}, u32[]{:S(2)}) %collective-permute-start) | collective-permute-done | bytes 2097184 | tf_op jit(solution)/shard_map/ppermute | solution.py:15
  22.0 0.5 add.9
  22.4 2.9 %collective-permute-start.1 = (f32[1024,512]{1,0:T(8,128)S(1)}, f32[1024,512]{1,0:T(8,128)S(1)}, u32[]{:S(2)}, u32[]{:S(2)}) collective-permute-start(f32[1024,512]{1,0:T(8,128)S(1)} %add.9), channel_id=1, source_target_pairs={{0,8},{4,12},{8,0},{12,4},{16,24},{20,28},{24,16},{28,20},{1,9},{5... | collective-permute-start | bytes 6291464 | tf_op jit(solution)/shard_map/ppermute | solution.py:15
  25.4 45.9 %collective-permute-done.1 = f32[1024,512]{1,0:T(8,128)S(1)} collective-permute-done((f32[1024,512]{1,0:T(8,128)S(1)}, f32[1024,512]{1,0:T(8,128)S(1)}, u32[]{:S(2)}, u32[]{:S(2)}) %collective-permute-start.1) | collective-permute-done | bytes 2097184 | tf_op jit(solution)/shard_map/ppermute | solution.py:15
  71.3 0.5 add.10
  71.8 1.8 %collective-permute-start.2 = (f32[1024,512]{1,0:T(8,128)S(1)}, f32[1024,512]{1,0:T(8,128)S(1)}, u32[]{:S(2)}, u32[]{:S(2)}) collective-permute-start(f32[1024,512]{1,0:T(8,128)S(1)} %add.10), channel_id=1, source_target_pairs={{0,16},{4,20},{8,24},{12,28},{16,0},{20,4},{24,8},{28,12},{1,17},{... | collective-permute-start | bytes 6291464 | tf_op jit(solution)/shard_map/ppermute | solution.py:15
  73.6 45.3 %collective-permute-done.2 = f32[1024,512]{1,0:T(8,128)S(1)} collective-permute-done((f32[1024,512]{1,0:T(8,128)S(1)}, f32[1024,512]{1,0:T(8,128)S(1)}, u32[]{:S(2)}, u32[]{:S(2)}) %collective-permute-start.2) | collective-permute-done | bytes 2097184 | tf_op jit(solution)/shard_map/ppermute | solution.py:15
  118.9 8.5 %fusion = f32[16,128,512]{2,1,0:T(8,128)} fusion(s32[16,128]{1,0:T(8,128)S(1)} %broadcast_subtract_fusion, f32[1024,512]{1,0:T(8,128)S(1)} %add.10, f32[1024,512]{1,0:T(8,128)S(1)} %collective-permute-done.2), kind=kOutput, calls=%fused_computation.1 | convolution fusion | flops 12887523328 | bytes 8396800 | tf_op jit(solution)/shard_map/gkn,nb->gkb/dot_general | solution.py:28
Async XLA Ops:
  17.6 4.3 %collective-permute-start = (f32[1024,512]{1,0:T(8,128)S(1)}, f32[1024,512]{1,0:T(8,128)S(1)}, u32[]{:S(2)}, u32[]{:S(2)}) collective-permute-start(f32[1024,512]{1,0:T(8,128)S(1)} %fusion.8), channel_id=1, source_target_pairs={{0,4},{4,0},{8,12},{12,8},{16,20},{20,16},{24,28},{28,24},{1,5},{5... | collective-permute-start | bytes 6291464 | tf_op jit(solution)/shard_map/ppermute | solution.py:15
  22.4 48.8 %collective-permute-start.1 = (f32[1024,512]{1,0:T(8,128)S(1)}, f32[1024,512]{1,0:T(8,128)S(1)}, u32[]{:S(2)}, u32[]{:S(2)}) collective-permute-start(f32[1024,512]{1,0:T(8,128)S(1)} %add.9), channel_id=1, source_target_pairs={{0,8},{4,12},{8,0},{12,4},{16,24},{20,28},{24,16},{28,20},{1,9},{5... | collective-permute-start | bytes 6291464 | tf_op jit(solution)/shard_map/ppermute | solution.py:15
  71.8 47.2 %collective-permute-start.2 = (f32[1024,512]{1,0:T(8,128)S(1)}, f32[1024,512]{1,0:T(8,128)S(1)}, u32[]{:S(2)}, u32[]{:S(2)}) collective-permute-start(f32[1024,512]{1,0:T(8,128)S(1)} %add.10), channel_id=1, source_target_pairs={{0,16},{4,20},{8,24},{12,28},{16,0},{20,4},{24,8},{28,12},{1,17},{... | collective-permute-start | bytes 6291464 | tf_op jit(solution)/shard_map/ppermute | solution.py:15
